TPU v7x, 256 devices: a whole 4x4x8 slice. The times are simulated.
256 devices in a mesh: dp: 8 (over z), vocab: 32 (over x, y, core).
Axes of the slice: x: 4, y: 4, z: 8, core: 2. Of those that a mesh axis runs over, the one named last changes fastest.
Arguments:
- token_ids: int32 [65536], P(('dp', 'vocab')), may hold values from 0 to 152063, as said below
- token_count: int32 [256], P(('dp', 'vocab')), may hold values from 16 to 256
- out_grads: bfloat16 [65536, 5120], P(('dp', 'vocab')), may hold values from -18 to 18
- master_rows: float32 [16384, 5120], P('vocab', 'dp'), may hold values from -0.8 to 0.8
- first_moment: float32 [16384, 5120], P('vocab', 'dp'), may hold values from -4 to 4
- second_moment: float32 [16384, 5120], P('vocab', 'dp'), may hold values from 0.001 to 1
Outputs:
- new_master: float32 [16384, 5120], P('vocab', 'dp')
- new_first: float32 [16384, 5120], P('vocab', 'dp')
- new_second: float32 [16384, 5120], P('vocab', 'dp')
- table_rows: bfloat16 [16384, 5120], P('vocab')
Inputs may be any that keep to these rules, and one draw needn't show every extreme that they name: `token_ids`: within each block of 256 slots, among the live slots (the first token_count of the block) at most 8 have ids in the new rows j * 512 + 135680 to (j + 1) * 512 + 135679 for any one j, and for some j exactly 8 in every block. Slots past token_count hold ids of new rows that are to be ignored.
All inputs are finite; a program needn't handle non-finite values.
Results may differ from a plain program's by a relative error of at most 0.001.
Values may be sent and summed in bfloat16 or wider, within the bound.
No kernel may reach another device: no remote copies, remote signals or barrier semaphores. Data moves between devices by JAX's collectives and lax.ppermute only.
A program may use at most 64 MiB of HBM per device.

v0:
```python
import jax
import jax.numpy as jnp
from jax import lax
from jax.sharding import PartitionSpec as P

VOCAB = 152064
CAP = 8
beta_one = 0.9
beta_two = 0.999
corr_one = 1.0 - 0.9**10
corr_two = 1.0 - 0.999**10
learn_rate = 0.01
epsilon = 1e-08


def body(token_ids, token_count, out_grads, master_rows, first_moment, second_moment):
    owners = lax.axis_size("vocab")
    groups = lax.axis_size("dp")
    rows_own = master_rows.shape[0]
    tok_slots = token_ids.shape[0]
    first_new = VOCAB - rows_own * owners
    position = jnp.arange(tok_slots)
    is_live = (position < token_count[0]) & (token_ids >= first_new)
    new_index = token_ids - first_new
    owner_of = new_index // rows_own
    row_in_owner = new_index % rows_own
    belongs = (owner_of[:, None] == jnp.arange(owners)[None, :]) & is_live[:, None]
    ranking = jnp.cumsum(belongs.astype(jnp.int32), axis=0) - 1
    my_rank = jnp.sum(jnp.where(belongs, ranking, 0), axis=1)
    slot_index = jnp.where(is_live, owner_of * CAP + my_rank, -1)
    placing = jnp.arange(owners * CAP)[:, None] == slot_index[None, :]
    outgoing = jnp.dot(
        placing.astype(jnp.bfloat16), out_grads, preferred_element_type=jnp.float32
    ).astype(jnp.bfloat16)
    slot_row = jnp.max(jnp.where(placing, row_in_owner[None, :], -1), axis=1)
    upper_part = jnp.where(slot_row >= 0, slot_row // 16, -1)
    lower_part = jnp.where(slot_row >= 0, slot_row % 16, 0)
    row_pairs = jnp.stack([upper_part, lower_part], axis=1).astype(jnp.bfloat16)
    tiled_pairs = jnp.tile(row_pairs, (1, groups))
    split_grads, split_pairs = (
        lax.all_to_all(outgoing, "dp", split_axis=1, concat_axis=0, tiled=True),
        lax.all_to_all(tiled_pairs, "dp", split_axis=1, concat_axis=0, tiled=True),
    )
    split_grads = split_grads.reshape(groups, owners * CAP, split_grads.shape[1])
    split_pairs = split_pairs.reshape(groups, owners * CAP, 2)
    arrived, arrived_pairs = (
        lax.all_to_all(split_grads, "vocab", split_axis=1, concat_axis=0, tiled=True),
        lax.all_to_all(split_pairs, "vocab", split_axis=1, concat_axis=0, tiled=True),
    )
    arrived = arrived.reshape(-1, arrived.shape[2])
    arrived_pairs = arrived_pairs.reshape(-1, 2).astype(jnp.float32)
    decoded = arrived_pairs[:, 0] * 16.0 + arrived_pairs[:, 1]
    selector = decoded[None, :] == jnp.arange(rows_own, dtype=jnp.float32)[:, None]
    gradient = jnp.dot(selector.astype(jnp.bfloat16), arrived, preferred_element_type=jnp.float32)
    new_first = beta_one * first_moment + (1.0 - beta_one) * gradient
    new_second = beta_two * second_moment + (1.0 - beta_two) * gradient * gradient
    update = new_first / corr_one / (jnp.sqrt(new_second / corr_two) + epsilon)
    new_master = master_rows - learn_rate * update
    table_rows = lax.all_gather(new_master.astype(jnp.bfloat16), "dp", axis=1, tiled=True)
    return (new_master, new_first, new_second, table_rows)


def solution(mesh):
    return jax.shard_map(
        body,
        mesh=mesh,
        in_specs=(
            P(("dp", "vocab")),
            P(("dp", "vocab")),
            P(("dp", "vocab"), None),
            P("vocab", "dp"),
            P("vocab", "dp"),
            P("vocab", "dp"),
        ),
        out_specs=(P("vocab", "dp"), P("vocab", "dp"), P("vocab", "dp"), P("vocab", None)),
        check_vma=False,
    )
```

profile of v0, /device:TPU:1, one launch (start us, length us, event | category | flops | bytes accessed | tf_op | source)
XLA Modules:
  0.0 226.1 jit_solution(13173120727746846813)
XLA Ops:
  8.0 0.7 and_select_fusion.2
  8.7 0.7 fusion.15
  9.4 0.7 compare_and_fusion
  10.0 0.6 reduce-window.6
  11.0 0.7 add_select_fusion
  11.8 0.6 tile.2
  12.4 9.0 %all-to-all-start = ((bf16[256,8,2]{0,2,1:T(2,128)(2,1)}), bf16[256,8,2]{0,2,1:T(2,128)(2,1)S(1)}, u32[]{:S(2)}, u32[]{:S(2)}) async-start(bf16[256,8,2]{0,2,1:T(2,128)(2,1)} %tile.2), calls=%async_computation | async-start | bytes 16384 | tf_op jit(solution)/shard_map/all_to_all | solution.py:42
  21.4 0.8 convolution_convert_fusion
  22.3 1.7 copy.51
  24.0 4.0 %all-to-all-done = bf16[256,8,2]{0,2,1:T(2,128)(2,1)S(1)} async-done(((bf16[256,8,2]{0,2,1:T(2,128)(2,1)}), bf16[256,8,2]{0,2,1:T(2,128)(2,1)S(1)}, u32[]{:S(2)}, u32[]{:S(2)}) %all-to-all-start) | async-done | bytes 8224 | tf_op jit(solution)/shard_map/all_to_all | solution.py:42
  28.0 4.4 %all-to-all-start.2 = ((bf16[256,8,640]{2,0,1:T(8,128)(2,1)}), bf16[256,8,640]{2,0,1:T(8,128)(2,1)}, u32[]{:S(2)}, u32[]{:S(2)}) async-start(bf16[256,8,640]{2,0,1:T(8,128)(2,1)} %bitcast.43), calls=%async_computation.2 | async-start | bytes 5242880 | tf_op jit(solution)/shard_map/all_to_all | solution.py:41
  32.4 0.8 copy.39
  33.2 58.8 %all-to-all-done.2 = bf16[256,8,640]{2,0,1:T(8,128)(2,1)} async-done(((bf16[256,8,640]{2,0,1:T(8,128)(2,1)}), bf16[256,8,640]{2,0,1:T(8,128)(2,1)}, u32[]{:S(2)}, u32[]{:S(2)}) %all-to-all-start.2) | async-done | bytes 2621472 | tf_op jit(solution)/shard_map/all_to_all | solution.py:41
  92.0 10.9 %all-to-all-start.1 = ((bf16[8,256,2]{0,2,1:T(2,128)(2,1)}), bf16[8,256,2]{0,2,1:T(2,128)(2,1)S(1)}, u32[]{:S(2)}, u32[]{:S(2)}) async-start(bf16[8,256,2]{0,2,1:T(2,128)(2,1)} %copy.39), calls=%async_computation.1 | async-start | bytes 262144 | tf_op jit(solution)/shard_map/all_to_all | solution.py:48
  103.0 4.7 %copy.43 = bf16[8,256,640]{2,0,1:T(8,128)(2,1)} copy(bf16[8,256,640]{2,1,0:T(8,128)(2,1)} %bitcast.8) | data formatting | bytes 5242880 | tf_op jit(solution)/shard_map/all_to_all | solution.py:41
  107.7 2.9 %all-to-all-done.1 = bf16[8,256,2]{0,2,1:T(2,128)(2,1)S(1)} async-done(((bf16[8,256,2]{0,2,1:T(2,128)(2,1)}), bf16[8,256,2]{0,2,1:T(2,128)(2,1)S(1)}, u32[]{:S(2)}, u32[]{:S(2)}) %all-to-all-start.1) | async-done | bytes 8224 | tf_op jit(solution)/shard_map/all_to_all | solution.py:48
  110.7 4.8 %all-to-all-start.3 = ((bf16[8,256,640]{2,0,1:T(8,128)(2,1)}), bf16[8,256,640]{2,0,1:T(8,128)(2,1)}, u32[]{:S(2)}, u32[]{:S(2)}) async-start(bf16[8,256,640]{2,0,1:T(8,128)(2,1)} %copy.43), calls=%async_computation.3 | async-start | bytes 5242880 | tf_op jit(solution)/shard_map/all_to_all | solution.py:47
  115.6 0.2 reshape.169
  116.1 33.4 %all-to-all-done.3 = bf16[8,256,640]{2,0,1:T(8,128)(2,1)} async-done(((bf16[8,256,640]{2,0,1:T(8,128)(2,1)}), bf16[8,256,640]{2,0,1:T(8,128)(2,1)}, u32[]{:S(2)}, u32[]{:S(2)}) %all-to-all-start.3) | async-done | bytes 2621472 | tf_op jit(solution)/shard_map/all_to_all | solution.py:47
  149.5 2.4 %copy.45 = bf16[32,8,8,640]{3,2,1,0:T(8,128)(2,1)S(1)} copy(bf16[32,8,8,640]{3,1,2,0:T(8,128)(2,1)} %bitcast.11) | data formatting | bytes 5242880 | tf_op jit(solution)/shard_map/all_to_all | solution.py:47
  152.0 0.4 copy-done.3
  152.4 4.7 %fusion.11 = (bf16[512,640]{1,0:T(8,128)(2,1)}, f32[512,640]{1,0:T(8,128)}, f32[512,640]{1,0:T(8,128)}, f32[512,640]{1,0:T(8,128)}) fusion(f32[512,640]{1,0:T(8,128)S(1)} %copy-done.1, f32[512,640]{1,0:T(8,128)S(1)} %copy-done.2, f32[512,640]{1,0:T(8,128)S(1)} %copy-done.3, bf16[2048,640]{1,0:T(8,128)(2,1)S(1)} %bitcast.45, f32[2048]{0:T(1024)S(1)} %bitcast.49), kind=kOutput, calls=%fused_computation.43 | convolution fusion | flops 1347813376 | bytes 11149312 | tf_op jit(solution)/shard_map/dot_general | solution.py:54
  157.1 57.0 %all-gather.2.cloned.1.call-done = bf16[512,5120]{1,0:T(8,128)(2,1)} async-done(((bf16[512,640]{1,0:T(8,128)(2,1)}), bf16[512,5120]{1,0:T(8,128)(2,1)}) %all-gather.2.cloned.1.call-update) | async-done | bytes 5242896 | tf_op jit(solution)/shard_map/all_gather | solution.py:59
  214.1 5.2 %copy.54 = bf16[512,5120]{1,0:T(8,128)(2,1)} copy(bf16[512,5120]{1,0:T(8,128)(2,1)} %all-gather.2.cloned.1.call-done) | data formatting | bytes 10485760
  (21 shorter events, 1.1 us)
Async XLA Ops:
  7.2 14.3 %copy-start = (bf16[256,5120]{1,0:T(8,128)(2,1)S(1)}, bf16[256,5120]{1,0:T(8,128)(2,1)}, u32[]{:S(2)}) copy-start(bf16[256,5120]{1,0:T(8,128)(2,1)} %param.8) | copy-start | bytes 7864324
  12.4 15.6 %all-to-all-start = ((bf16[256,8,2]{0,2,1:T(2,128)(2,1)}), bf16[256,8,2]{0,2,1:T(2,128)(2,1)S(1)}, u32[]{:S(2)}, u32[]{:S(2)}) async-start(bf16[256,8,2]{0,2,1:T(2,128)(2,1)} %tile.2), calls=%async_computation | async-start | bytes 16384 | tf_op jit(solution)/shard_map/all_to_all | solution.py:42
  28.0 64.0 %all-to-all-start.2 = ((bf16[256,8,640]{2,0,1:T(8,128)(2,1)}), bf16[256,8,640]{2,0,1:T(8,128)(2,1)}, u32[]{:S(2)}, u32[]{:S(2)}) async-start(bf16[256,8,640]{2,0,1:T(8,128)(2,1)} %bitcast.43), calls=%async_computation.2 | async-start | bytes 5242880 | tf_op jit(solution)/shard_map/all_to_all | solution.py:41
  92.0 18.6 %all-to-all-start.1 = ((bf16[8,256,2]{0,2,1:T(2,128)(2,1)}), bf16[8,256,2]{0,2,1:T(2,128)(2,1)S(1)}, u32[]{:S(2)}, u32[]{:S(2)}) async-start(bf16[8,256,2]{0,2,1:T(2,128)(2,1)} %copy.39), calls=%async_computation.1 | async-start | bytes 262144 | tf_op jit(solution)/shard_map/all_to_all | solution.py:48
  110.7 38.9 %all-to-all-start.3 = ((bf16[8,256,640]{2,0,1:T(8,128)(2,1)}), bf16[8,256,640]{2,0,1:T(8,128)(2,1)}, u32[]{:S(2)}, u32[]{:S(2)}) async-start(bf16[8,256,640]{2,0,1:T(8,128)(2,1)} %copy.43), calls=%async_computation.3 | async-start | bytes 5242880 | tf_op jit(solution)/shard_map/all_to_all | solution.py:47
  115.4 98.7 %all-gather.2.cloned.1.call-start = ((), (), s32[]{:S(2)}) async-start(), calls=%async_computation.4 | async-start | bytes 5898240 | tf_op jit(solution)/shard_map/all_gather | solution.py:59
  149.5 2.4 %copy-start.1 = (f32[512,640]{1,0:T(8,128)S(1)}, f32[512,640]{1,0:T(8,128)}, u32[]{:S(2)}) copy-start(f32[512,640]{1,0:T(8,128)} %param.9) | copy-start | bytes 3932164
  149.5 2.5 %copy-start.2 = (f32[512,640]{1,0:T(8,128)S(1)}, f32[512,640]{1,0:T(8,128)}, u32[]{:S(2)}) copy-start(f32[512,640]{1,0:T(8,128)} %param.10) | copy-start | bytes 3932164
  149.5 2.9 %copy-start.3 = (f32[512,640]{1,0:T(8,128)S(1)}, f32[512,640]{1,0:T(8,128)}, u32[]{:S(2)}) copy-start(f32[512,640]{1,0:T(8,128)} %param.11) | copy-start | bytes 3932164
Sparse Core Ops, SparseCore 0:
  157.2 56.8 all-gather.1
where the time goes:
time: 227 us; the launch traced here: 226 us
  waiting for transfers between devices  156 us (69%)
  starting transfers between devices  29.2 us (13%)
  local copies, waits for them, and re-layouts  16.7 us (7%)
  between operations  14.9 us (7%)
  matrix products  5.52 us (2%)
  other arithmetic  3.65 us (2%)
    all_to_all x1, waiting for transfers between devices, body(): lax.all_to_all(outgoing, 'dp', split_axis=1, concat_axis=0, tiled=True)  58.8 us
    all_gather x1, waiting for transfers between devices, body(): lax.all_gather(new_master.astype(jnp.bfloat16), 'dp', axis=1, tiled=True)  57 us
    all_to_all x1, waiting for transfers between devices, body(): lax.all_to_all(split_grads, 'vocab', split_axis=1, concat_axis=0, tiled=T...  33.4 us
    all_to_all x1, starting transfers between devices, body(): lax.all_to_all(split_pairs, 'vocab', split_axis=1, concat_axis=0, tiled=T...  10.9 us
    all_to_all x1, starting transfers between devices, body(): lax.all_to_all(tiled_pairs, 'dp', split_axis=1, concat_axis=0, tiled=True)  9 us
    all_to_all x2, local copies, waits for them, and re-layouts, body(): lax.all_to_all(outgoing, 'dp', split_axis=1, concat_axis=0, tiled=True)  6.47 us
    unnamed x9, local copies, waits for them, and re-layouts  5.69 us
    all_to_all x1, starting transfers between devices, body(): lax.all_to_all(split_grads, 'vocab', split_axis=1, concat_axis=0, tiled=T...  4.79 us
  transfers between devices with their start and end apart: 5, of which 5 were waited for; matrix products, arithmetic and copies ran while one was open for 4% of the time, Pallas kernels for 0%

commit v1 on v0

--- a/solution.py
+++ b/solution.py
@@ -56,7 +56,12 @@
     new_second = beta_two * second_moment + (1.0 - beta_two) * gradient * gradient
     update = new_first / corr_one / (jnp.sqrt(new_second / corr_two) + epsilon)
     new_master = master_rows - learn_rate * update
-    table_rows = lax.all_gather(new_master.astype(jnp.bfloat16), "dp", axis=1, tiled=True)
+    table_rows = jnp.concatenate(
+        lax.all_to_all(
+            jnp.stack([new_master.astype(jnp.bfloat16)] * lax.axis_size("dp")), "dp", 0, 0
+        ),
+        axis=1,
+    )
     return (new_master, new_first, new_second, table_rows)
 
 

time: 227 us -> 288 us (1.27)
  blocking collectives: 0 us -> 121 us
  waiting for transfers between devices: 156 us -> 99.2 us
  between operations: 14.9 us -> 1.55 us
  local copies, waits for them, and re-layouts: 16.7 us -> 27.7 us
    all_to_all x0 -> x1, blocking collectives: none -> 121 us  [body(): lax.all_to_all(jnp.stack([new_master.astype(jnp.bfloat16)] * lax.axis_siz...]
    all_gather x1 -> x0, waiting for transfers between devices: 57 us -> none  [body(): lax.all_gather(new_master.astype(jnp.bfloat16), 'dp', axis=1, tiled=True)]
    all_to_all x0 -> x1, local copies, waits for them, and re-layouts: none -> 7.87 us  [body(): lax.all_to_all(jnp.stack([new_master.astype(jnp.bfloat16)] * lax.axis_siz...]
  transfers between devices with their start and end apart: 5 -> 4, of which waited for: 5 -> 4; matrix products, arithmetic and copies ran while one was open for 4% -> 3% of each run, Pallas kernels for 0% -> 0%
where the time goes in v1:
time: 288 us; the launch traced here: 287 us
  blocking collectives  121 us (42%)
  waiting for transfers between devices  99.2 us (34%)
  starting transfers between devices  29.1 us (10%)
  local copies, waits for them, and re-layouts  27.7 us (10%)
  matrix products  5.31 us (2%)
  other arithmetic  3.65 us (1%)
    all_to_all x1, blocking collectives, body(): lax.all_to_all(jnp.stack([new_master.astype(jnp.bfloat16)] * lax.axis_siz...  121 us
    all_to_all x1, waiting for transfers between devices, body(): lax.all_to_all(outgoing, 'dp', split_axis=1, concat_axis=0, tiled=True)  58.8 us
    all_to_all x1, waiting for transfers between devices, body(): lax.all_to_all(split_grads, 'vocab', split_axis=1, concat_axis=0, tiled=T...  33.5 us
    all_to_all x1, starting transfers between devices, body(): lax.all_to_all(split_pairs, 'vocab', split_axis=1, concat_axis=0, tiled=T...  10.9 us
    all_to_all x1, starting transfers between devices, body(): lax.all_to_all(tiled_pairs, 'dp', split_axis=1, concat_axis=0, tiled=True)  9 us
    unnamed x9, local copies, waits for them, and re-layouts  8.42 us
    all_to_all x1, local copies, waits for them, and re-layouts, body(): lax.all_to_all(jnp.stack([new_master.astype(jnp.bfloat16)] * lax.axis_siz...  7.87 us
    all_to_all x2, local copies, waits for them, and re-layouts, body(): lax.all_to_all(outgoing, 'dp', split_axis=1, concat_axis=0, tiled=True)  6.47 us
  transfers between devices with their start and end apart: 4, of which 4 were waited for; matrix products, arithmetic and copies ran while one was open for 3% of the time, Pallas kernels for 0%

profile of v1, /device:TPU:1, one launch (start us, length us, event | category | flops | bytes accessed | tf_op | source)
XLA Modules:
  0.0 287.1 jit_solution(15472980525736258792)
XLA Ops:
  1.4 0.7 and_select_fusion.2
  2.1 0.7 fusion.15
  2.8 0.7 compare_and_fusion
  3.5 0.6 reduce-window.6
  4.4 0.7 add_select_fusion
  5.3 0.6 tile.2
  5.9 9.0 %all-to-all-start = ((bf16[256,8,2]{0,2,1:T(2,128)(2,1)}), bf16[256,8,2]{0,2,1:T(2,128)(2,1)S(1)}, u32[]{:S(2)}, u32[]{:S(2)}) async-start(bf16[256,8,2]{0,2,1:T(2,128)(2,1)} %tile.2), calls=%async_computation | async-start | bytes 16384 | tf_op jit(solution)/shard_map/all_to_all | solution.py:42
  14.9 0.8 convolution_convert_fusion
  15.8 1.7 copy.65
  17.5 4.0 %all-to-all-done = bf16[256,8,2]{0,2,1:T(2,128)(2,1)S(1)} async-done(((bf16[256,8,2]{0,2,1:T(2,128)(2,1)}), bf16[256,8,2]{0,2,1:T(2,128)(2,1)S(1)}, u32[]{:S(2)}, u32[]{:S(2)}) %all-to-all-start) | async-done | bytes 8224 | tf_op jit(solution)/shard_map/all_to_all | solution.py:42
  21.5 4.4 %all-to-all-start.2 = ((bf16[256,8,640]{2,0,1:T(8,128)(2,1)}), bf16[256,8,640]{2,0,1:T(8,128)(2,1)}, u32[]{:S(2)}, u32[]{:S(2)}) async-start(bf16[256,8,640]{2,0,1:T(8,128)(2,1)} %bitcast.47), calls=%async_computation.2 | async-start | bytes 5242880 | tf_op jit(solution)/shard_map/all_to_all | solution.py:41
  25.9 0.8 copy.51
  26.7 58.8 %all-to-all-done.2 = bf16[256,8,640]{2,0,1:T(8,128)(2,1)} async-done(((bf16[256,8,640]{2,0,1:T(8,128)(2,1)}), bf16[256,8,640]{2,0,1:T(8,128)(2,1)}, u32[]{:S(2)}, u32[]{:S(2)}) %all-to-all-start.2) | async-done | bytes 2621472 | tf_op jit(solution)/shard_map/all_to_all | solution.py:41
  85.5 10.9 %all-to-all-start.1 = ((bf16[8,256,2]{0,2,1:T(2,128)(2,1)}), bf16[8,256,2]{0,2,1:T(2,128)(2,1)S(1)}, u32[]{:S(2)}, u32[]{:S(2)}) async-start(bf16[8,256,2]{0,2,1:T(2,128)(2,1)} %copy.51), calls=%async_computation.1 | async-start | bytes 262144 | tf_op jit(solution)/shard_map/all_to_all | solution.py:48
  96.4 4.7 %copy.55 = bf16[8,256,640]{2,0,1:T(8,128)(2,1)} copy(bf16[8,256,640]{2,1,0:T(8,128)(2,1)} %bitcast.8) | data formatting | bytes 5242880 | tf_op jit(solution)/shard_map/all_to_all | solution.py:41
  101.2 2.9 %all-to-all-done.1 = bf16[8,256,2]{0,2,1:T(2,128)(2,1)S(1)} async-done(((bf16[8,256,2]{0,2,1:T(2,128)(2,1)}), bf16[8,256,2]{0,2,1:T(2,128)(2,1)S(1)}, u32[]{:S(2)}, u32[]{:S(2)}) %all-to-all-start.1) | async-done | bytes 8224 | tf_op jit(solution)/shard_map/all_to_all | solution.py:48
  104.1 4.8 %all-to-all-start.3 = ((bf16[8,256,640]{2,0,1:T(8,128)(2,1)}), bf16[8,256,640]{2,0,1:T(8,128)(2,1)}, u32[]{:S(2)}, u32[]{:S(2)}) async-start(bf16[8,256,640]{2,0,1:T(8,128)(2,1)} %copy.55), calls=%async_computation.3 | async-start | bytes 5242880 | tf_op jit(solution)/shard_map/all_to_all | solution.py:47
  109.5 33.5 %all-to-all-done.3 = bf16[8,256,640]{2,0,1:T(8,128)(2,1)} async-done(((bf16[8,256,640]{2,0,1:T(8,128)(2,1)}), bf16[8,256,640]{2,0,1:T(8,128)(2,1)}, u32[]{:S(2)}, u32[]{:S(2)}) %all-to-all-start.3) | async-done | bytes 2621472 | tf_op jit(solution)/shard_map/all_to_all | solution.py:47
  143.0 2.4 copy.57
  145.9 4.5 %fusion.11 = (bf16[512,640]{1,0:T(8,128)(2,1)S(1)}, f32[512,640]{1,0:T(8,128)}, f32[512,640]{1,0:T(8,128)}, f32[512,640]{1,0:T(8,128)}) fusion(f32[512,640]{1,0:T(8,128)S(1)} %copy-done.1, f32[512,640]{1,0:T(8,128)S(1)} %copy-done.2, f32[512,640]{1,0:T(8,128)S(1)} %copy-done.3, bf16[2048,640]{1,0:T(8,128)(2,1)S(1)} %bitcast.49, f32[2048]{0:T(1024)S(1)} %bitcast.53), kind=kOutput, calls=%fused_computation.43 | convolution fusion | flops 1347813376 | bytes 11149312 | tf_op jit(solution)/shard_map/dot_general | solution.py:54
  150.3 0.4 stack.5
  150.7 120.6 %all_to_all.58 = bf16[8,512,640]{2,1,0:T(8,128)(2,1)} all-to-all(bf16[8,512,640]{2,1,0:T(8,128)(2,1)S(1)} %stack.5), channel_id=1, replica_groups=mesh['dp'=8,'vocab'=32] {'dp'}, dimensions={0} | all-to-all | bytes 10485760 | tf_op jit(solution)/shard_map/all_to_all | solution.py:60
  271.4 7.9 %copy.58 = bf16[8,512,640]{1,2,0:T(8,128)(2,1)} copy(bf16[8,512,640]{2,1,0:T(8,128)(2,1)} %all_to_all.58) | data formatting | bytes 10485760 | tf_op jit(solution)/shard_map/all_to_all | solution.py:60
  279.2 7.9 %copy.59 = bf16[512,5120]{1,0:T(8,128)(2,1)} copy(bf16[512,5120]{0,1:T(8,128)(2,1)} %bitcast.46) | data formatting | bytes 10485760
  (21 shorter events, 1.6 us)
Async XLA Ops:
  0.6 14.3 %copy-start = (bf16[256,5120]{1,0:T(8,128)(2,1)S(1)}, bf16[256,5120]{1,0:T(8,128)(2,1)}, u32[]{:S(2)}) copy-start(bf16[256,5120]{1,0:T(8,128)(2,1)} %param.8) | copy-start | bytes 7864324
  5.9 15.6 %all-to-all-start = ((bf16[256,8,2]{0,2,1:T(2,128)(2,1)}), bf16[256,8,2]{0,2,1:T(2,128)(2,1)S(1)}, u32[]{:S(2)}, u32[]{:S(2)}) async-start(bf16[256,8,2]{0,2,1:T(2,128)(2,1)} %tile.2), calls=%async_computation | async-start | bytes 16384 | tf_op jit(solution)/shard_map/all_to_all | solution.py:42
  21.5 64.0 %all-to-all-start.2 = ((bf16[256,8,640]{2,0,1:T(8,128)(2,1)}), bf16[256,8,640]{2,0,1:T(8,128)(2,1)}, u32[]{:S(2)}, u32[]{:S(2)}) async-start(bf16[256,8,640]{2,0,1:T(8,128)(2,1)} %bitcast.47), calls=%async_computation.2 | async-start | bytes 5242880 | tf_op jit(solution)/shard_map/all_to_all | solution.py:41
  85.5 18.6 %all-to-all-start.1 = ((bf16[8,256,2]{0,2,1:T(2,128)(2,1)}), bf16[8,256,2]{0,2,1:T(2,128)(2,1)S(1)}, u32[]{:S(2)}, u32[]{:S(2)}) async-start(bf16[8,256,2]{0,2,1:T(2,128)(2,1)} %copy.51), calls=%async_computation.1 | async-start | bytes 262144 | tf_op jit(solution)/shard_map/all_to_all | solution.py:48
  104.1 38.9 %all-to-all-start.3 = ((bf16[8,256,640]{2,0,1:T(8,128)(2,1)}), bf16[8,256,640]{2,0,1:T(8,128)(2,1)}, u32[]{:S(2)}, u32[]{:S(2)}) async-start(bf16[8,256,640]{2,0,1:T(8,128)(2,1)} %copy.55), calls=%async_computation.3 | async-start | bytes 5242880 | tf_op jit(solution)/shard_map/all_to_all | solution.py:47
  143.0 2.4 copy-start.1
  143.0 2.5 copy-start.2
  143.0 2.9 %copy-start.3 = (f32[512,640]{1,0:T(8,128)S(1)}, f32[512,640]{1,0:T(8,128)}, u32[]{:S(2)}) copy-start(f32[512,640]{1,0:T(8,128)} %param.11) | copy-start | bytes 3932164
